TPU v7x, 32 devices: a whole 2x2x4 slice. The times are simulated.
32 devices in a mesh: dp: 2 (over x), row: 4 (over z), col: 4 (over y, core).
Axes of the slice: x: 2, y: 2, z: 4, core: 2. Of those that a mesh axis runs over, the one named last changes fastest.
Arguments:
- expand_gradient: bfloat16 [2, 4096, 5120], P('dp', 'row', 'col'), may hold values from -24 to 24, as said below
- expand_master: float32 [4096, 5120], P(('row', 'dp'), 'col'), may hold values from -0.12 to 0.12
- expand_rows: float32 [4096], P(('row', 'dp')), may hold values from 0.01 to 1
- expand_columns: float32 [5120], P('col'), may hold values from 0.01 to 1
- contract_gradient: bfloat16 [2, 5120, 4096], P('dp', 'row', 'col'), may hold values from -24 to 24, as said below
- contract_master: float32 [5120, 4096], P(('row', 'dp'), 'col'), may hold values from -0.12 to 0.12
- contract_rows: float32 [5120], P(('row', 'dp')), may hold values from 0.01 to 1
- contract_columns: float32 [4096], P('col'), may hold values from 0.01 to 1
- attend_gradient: bfloat16 [2, 4096, 4096], P('dp', 'row', 'col'), may hold values from -24 to 24, as said below
- attend_master: float32 [4096, 4096], P(('row', 'dp'), 'col'), may hold values from -0.12 to 0.12
- attend_rows: float32 [4096], P(('row', 'dp')), may hold values from 0.01 to 1
- attend_columns: float32 [4096], P('col'), may hold values from 0.01 to 1
Outputs:
- expand_updated: float32 [4096, 5120], P(('row', 'dp'), 'col')
- expand_weights: bfloat16 [4096, 5120], P('row', 'col')
- expand_rows_next: float32 [4096], P(('row', 'dp'))
- expand_columns_next: float32 [5120], P('col')
- expand_step: float32 [4096, 5120], P(('row', 'dp'), 'col')
- contract_updated: float32 [5120, 4096], P(('row', 'dp'), 'col')
- contract_weights: bfloat16 [5120, 4096], P('row', 'col')
- contract_rows_next: float32 [5120], P(('row', 'dp'))
- contract_columns_next: float32 [4096], P('col')
- contract_step: float32 [5120, 4096], P(('row', 'dp'), 'col')
- attend_updated: float32 [4096, 4096], P(('row', 'dp'), 'col')
- attend_weights: bfloat16 [4096, 4096], P('row', 'col')
- attend_rows_next: float32 [4096], P(('row', 'dp'))
- attend_columns_next: float32 [4096], P('col')
- attend_step: float32 [4096, 4096], P(('row', 'dp'), 'col')
Inputs may be any that keep to these rules, and one draw needn't show every extreme that they name: `expand_gradient`: each replica's gradient, of any scale from entry to entry. `contract_gradient`: each replica's gradient, of any scale from entry to entry. `attend_gradient`: each replica's gradient, of any scale from entry to entry.
All inputs are finite; a program needn't handle non-finite values.
Results may differ from a plain program's by a relative error of at most 0.0004.
Values may be sent and summed in bfloat16 or wider, within the bound.
A program may use at most 128 MiB of HBM per device.

v0:
```python
import jax
import jax.numpy as jnp
from jax import lax
from jax.sharding import PartitionSpec as P

tiny_square = 1e-30
decay_rate = 0.9
learn_rate = 0.01


def finish(update_raw, clip_total, master, full_size):
    clip_scale = jnp.maximum(1.0, jnp.sqrt(clip_total / full_size))
    step_taken = update_raw / clip_scale
    updated = master - learn_rate * step_taken
    weights = lax.all_gather(updated.astype(jnp.bfloat16), "dp", axis=0, tiled=True)
    return (updated, weights, step_taken)


def reduce_gradient(gradient, dp_count):
    received = lax.all_to_all(gradient, "dp", split_axis=1, concat_axis=0, tiled=True)
    summed = jnp.sum(received.astype(jnp.float32), axis=0)
    return summed / dp_count


def body(
    expand_gradient,
    expand_master,
    expand_rows,
    expand_columns,
    contract_gradient,
    contract_master,
    contract_rows,
    contract_columns,
    attend_gradient,
    attend_master,
    attend_rows,
    attend_columns,
):
    groups = (
        (expand_gradient, expand_master, expand_rows, expand_columns),
        (contract_gradient, contract_master, contract_rows, contract_columns),
        (attend_gradient, attend_master, attend_rows, attend_columns),
    )
    dp_count = lax.axis_size("dp")
    col_count = lax.axis_size("col")
    split_count = dp_count * lax.axis_size("row")
    means = []
    for gradient, master, row_stat, column_stat in groups:
        means.append(reduce_gradient(gradient, dp_count))
    squares = [mean_grad * mean_grad + tiny_square for mean_grad in means]
    row_parts = [jnp.sum(square_block, axis=1) for square_block in squares]
    column_parts = [jnp.sum(square_block, axis=0) for square_block in squares]
    heights = [mean_grad.shape[0] * split_count for mean_grad in means]
    widths = [mean_grad.shape[1] * col_count for mean_grad in means]
    outputs = []
    for which in range(3):
        row_total = lax.psum(row_parts[which], "col")
        rows_next = decay_rate * groups[which][2] + (1.0 - decay_rate) * row_total / widths[which]
        column_total, rows_sum = lax.psum((column_parts[which], jnp.sum(rows_next)), ("dp", "row"))
        columns_next = (
            decay_rate * groups[which][3] + (1.0 - decay_rate) * column_total / heights[which]
        )
        row_mean = rows_sum / heights[which]
        update_raw = means[which] * jnp.sqrt(
            row_mean / (rows_next[:, None] * columns_next[None, :])
        )
        clip_total = lax.psum(jnp.sum(update_raw * update_raw), ("dp", "row", "col"))
        updated, weights, step_taken = finish(
            update_raw, clip_total, groups[which][1], heights[which] * widths[which]
        )
        outputs.extend([updated, weights, rows_next, columns_next, step_taken])
    return tuple(outputs)


def solution(mesh):
    return jax.shard_map(
        body,
        mesh=mesh,
        in_specs=(
            P("dp", "row", "col"),
            P(("row", "dp"), "col"),
            P(("row", "dp")),
            P("col"),
            P("dp", "row", "col"),
            P(("row", "dp"), "col"),
            P(("row", "dp")),
            P("col"),
            P("dp", "row", "col"),
            P(("row", "dp"), "col"),
            P(("row", "dp")),
            P("col"),
        ),
        out_specs=(
            P(("row", "dp"), "col"),
            P("row", "col"),
            P(("row", "dp")),
            P("col"),
            P(("row", "dp"), "col"),
            P(("row", "dp"), "col"),
            P("row", "col"),
            P(("row", "dp")),
            P("col"),
            P(("row", "dp"), "col"),
            P(("row", "dp"), "col"),
            P("row", "col"),
            P(("row", "dp")),
            P("col"),
            P(("row", "dp"), "col"),
        ),
        check_vma=False,
    )
```

profile of v0, /device:TPU:0, one launch (start us, length us, event | category | flops | bytes accessed | tf_op | source)
XLA Modules:
  0.0 387.2 jit_solution(6910142270513207531)
XLA Ops:
  7.2 6.8 %copy.41 = bf16[1,1024,1024]{2,0,1:T(2,128)(2,1)} copy(bf16[1,1024,1024]{2,1,0:T(8,128)(2,1)} %param.20) | data formatting | bytes 4194304 | tf_op args[8]
  14.4 12.8 %reduce.2 = bf16[1024,1024]{1,0:T(8,128)(2,1)S(1)} reduce(bf16[1024,1,1024]{2,1,0:T(2,128)(2,1)} %bitcast.22, bf16[]{:T(256)} %broadcast.37), dimensions={1}, to_apply=%bitcast.17.reduce_sub_computation | reduce | bytes 4194306
  29.7 5.5 %all-to-all-start.2 = ((bf16[2,2,262144]{2,1,0:T(2,128)(2,1)}), bf16[2,2,262144]{2,1,0:T(2,128)(2,1)}, u32[]{:S(2)}, u32[]{:S(2)}) async-start(bf16[2,2,262144]{2,1,0:T(2,128)(2,1)} %reshape.58), calls=%async_computation.2 | async-start | bytes 4194304 | tf_op jit(solution)/shard_map/all_to_all | solution.py:20
  35.2 6.4 %copy.40 = bf16[1,1024,1280]{2,0,1:T(2,128)(2,1)} copy(bf16[1,1024,1280]{2,1,0:T(8,128)(2,1)S(1)} %copy-done.4) | data formatting | bytes 5242880 | tf_op args[0]
  41.6 26.6 %reduce = bf16[1024,1280]{1,0:T(8,128)(2,1)S(1)} reduce(bf16[1024,1,1280]{2,1,0:T(2,128)(2,1)} %bitcast.21, bf16[]{:T(256)} %broadcast.37), dimensions={1}, to_apply=%bitcast.16.reduce_sub_computation | reduce | bytes 5242882
  70.0 5.8 %all-to-all-start = ((bf16[2,2,327680]{2,1,0:T(2,128)(2,1)}), bf16[2,2,327680]{2,1,0:T(2,128)(2,1)}, u32[]{:S(2)}, u32[]{:S(2)}) async-start(bf16[2,2,327680]{2,1,0:T(2,128)(2,1)} %reshape.54), calls=%async_computation | async-start | bytes 5242880 | tf_op jit(solution)/shard_map/all_to_all | solution.py:20
  75.9 18.2 %copy.39 = bf16[1,1280,1024]{2,0,1:T(2,128)(2,1)} copy(bf16[1,1280,1024]{2,1,0:T(8,128)(2,1)S(1)} %copy-done.5) | data formatting | bytes 5242880 | tf_op args[4]
  94.1 15.6 %reduce.1 = bf16[1280,1024]{1,0:T(8,128)(2,1)S(1)} reduce(bf16[1280,1,1024]{2,1,0:T(2,128)(2,1)} %bitcast.18, bf16[]{:T(256)} %broadcast.37), dimensions={1}, to_apply=%bitcast.15.reduce_sub_computation | reduce | bytes 5242882
  112.6 4.1 %all-to-all-start.1 = ((bf16[2,2,327680]{2,1,0:T(2,128)(2,1)}), bf16[2,2,327680]{2,1,0:T(2,128)(2,1)S(1)}, u32[]{:S(2)}, u32[]{:S(2)}) async-start(bf16[2,2,327680]{2,1,0:T(2,128)(2,1)} %reshape.56), calls=%async_computation.1 | async-start | bytes 5242880 | tf_op jit(solution)/shard_map/all_to_all | solution.py:20
  116.9 4.3 %reshape.59 = bf16[1024,1,1024]{2,1,0:T(2,128)(2,1)} reshape(bf16[2,2,262144]{2,1,0:T(2,128)(2,1)} %all-to-all-done.2) | data formatting | bytes 4194304
  126.5 5.1 %reshape.55 = bf16[1024,1,1280]{2,1,0:T(2,128)(2,1)} reshape(bf16[2,2,327680]{2,1,0:T(2,128)(2,1)} %all-to-all-done) | data formatting | bytes 5242880
  137.0 11.3 %all-to-all-done.1 = bf16[2,2,327680]{2,1,0:T(2,128)(2,1)S(1)} async-done(((bf16[2,2,327680]{2,1,0:T(2,128)(2,1)}), bf16[2,2,327680]{2,1,0:T(2,128)(2,1)S(1)}, u32[]{:S(2)}, u32[]{:S(2)}) %all-to-all-start.1) | async-done | bytes 2621472 | tf_op jit(solution)/shard_map/all_to_all | solution.py:20
  148.3 3.7 reshape.57
  156.8 6.2 %all-reduce.2 = (f32[512]{0:T(512)S(1)}, f32[640]{0:T(1024)S(1)}, f32[512]{0:T(512)S(1)}) all-reduce(f32[512]{0:T(512)S(1)} %get-tuple-element.17, f32[640]{0:T(1024)S(1)} %get-tuple-element.15, f32[512]{0:T(512)S(1)} %get-tuple-element.19), channel_id=1, replica_groups=mesh['dp'=2,'row'=4,'col'=4] {'col'}, use_global_device_ids=true, to_apply=%region_2.0 | all-reduce | flops 1664 | bytes 13312 | tf_op jit(solution)/shard_map/psum | solution.py:57
  164.2 38.0 %all-reduce.1 = (f32[1280]{0:T(1024)S(1)}, f32[]{:T(128)}, f32[1024]{0:T(1024)S(1)}, f32[]{:T(128)}, f32[1024]{0:T(1024)S(1)}, /*index=5*/f32[]{:T(128)}) all-reduce(f32[1280]{0:T(1024)S(1)} %get-tuple-element.18, f32[]{:T(128)} %get-tuple-element.48, ...), channel_id=1, replica_groups=mesh['dp'=2,'row'=4,'col'=4] {'dp','row'}, use_global_device_ids=true, to_apply=%region_6.0 | all-reduce | flops 3331 | bytes 26648 | tf_op jit(solution)/shard_map/psum | solution.py:59
  204.2 3.8 multiply_reduce_fusion.1
  212.2 37.2 %all-reduce = (f32[]{:T(128)}, f32[]{:T(128)}, f32[]{:T(128)}) all-reduce(f32[]{:T(128)} %multiply_reduce_fusion.1, f32[]{:T(128)} %multiply_reduce_fusion, f32[]{:T(128)} %multiply_reduce_fusion.2), channel_id=1, replica_groups=mesh['dp'=2,'row'=4,'col'=4] {'dp','row','col'}, use_global_device_ids=true, to_apply=%region_8.0 | all-reduce | flops 3 | bytes 24 | tf_op jit(solution)/shard_map/psum | solution.py:67
  250.2 5.9 %fusion.6 = (bf16[512,1024]{1,0:T(8,128)(2,1)}, f32[512,1024]{1,0:T(8,128)}, f32[512,1024]{1,0:T(8,128)}) fusion(f32[512,1024]{1,0:T(8,128)} %param.21, f32[]{:T(128)S(6)} %max.11, f32[1024]{0:T(1024)S(1)} %multiply_add_fusion.4, f32[512]{0:T(512)S(1)} %get-tuple-element.77, f32[]{:T(128)S(6)} %div.136, f32[512,1024]{1,0:T(8,128)} %copy-done.1), kind=kLoop, calls=%fused_computation.30 | loop fusion | flops 4194304 | bytes 9443336 | tf_op jit(solution)/shard_map/convert_element_type | solution.py:15
  256.9 6.7 %fusion.8 = (bf16[512,1280]{1,0:T(8,128)(2,1)}, f32[512,1280]{1,0:T(8,128)}, f32[512,1280]{1,0:T(8,128)}) fusion(f32[512,1280]{1,0:T(8,128)} %param.13, f32[]{:T(128)S(6)} %max.9, f32[1280]{0:T(1024)S(1)} %multiply_add_fusion.3, f32[512]{0:T(512)S(1)} %get-tuple-element.67, f32[]{:T(128)S(6)} %div.112, f32[512,1280]{1,0:T(8,128)} %copy-done), kind=kLoop, calls=%fused_computation.32 | loop fusion | flops 5242880 | bytes 11803656 | tf_op jit(solution)/shard_map/convert_element_type | solution.py:15
  264.3 6.3 %fusion.7 = (bf16[640,1024]{1,0:T(8,128)(2,1)}, f32[640,1024]{1,0:T(8,128)}, f32[640,1024]{1,0:T(8,128)}) fusion(f32[640,1024]{1,0:T(8,128)} %param.17, f32[]{:T(128)S(6)} %max.10, f32[1024]{0:T(1024)S(1)} %multiply_add_fusion.5, f32[640]{0:T(1024)S(1)} %get-tuple-element.72, f32[]{:T(128)S(6)} %div.124, f32[640,1024]{1,0:T(8,128)S(1)} %convert_reduce_fusion), kind=kLoop, calls=%fused_computation.31 | loop fusion | flops 5242880 | bytes 11803144 | tf_op jit(solution)/shard_map/convert_element_type | solution.py:15
  270.6 20.2 %all-gather.8.cloned.1.call-done = bf16[1024,1024]{1,0:T(8,128)(2,1)} async-done(((bf16[512,1024]{1,0:T(8,128)(2,1)}), bf16[1024,1024]{1,0:T(8,128)(2,1)}) %all-gather.8.cloned.1.call-update) | async-done | bytes 2097168 | tf_op jit(solution)/shard_map/all_gather | solution.py:15
  290.7 41.1 %all-gather.4.cloned.1.call-done = bf16[1024,1280]{1,0:T(8,128)(2,1)} async-done(((bf16[512,1280]{1,0:T(8,128)(2,1)}), bf16[1024,1280]{1,0:T(8,128)(2,1)}) %all-gather.4.cloned.1.call-update) | async-done | bytes 2621456 | tf_op jit(solution)/shard_map/all_gather | solution.py:15
  331.9 41.2 %all-gather.6.cloned.1.call-done = bf16[1280,1024]{1,0:T(8,128)(2,1)} async-done(((bf16[640,1024]{1,0:T(8,128)(2,1)}), bf16[1280,1024]{1,0:T(8,128)(2,1)}) %all-gather.6.cloned.1.call-update) | async-done | bytes 2621456 | tf_op jit(solution)/shard_map/all_gather | solution.py:15
  373.1 3.5 copy.45
  (68 shorter events, 32.8 us)
Async XLA Ops:
  29.7 5.5 %copy-start.4 = (bf16[1,1024,1280]{2,1,0:T(8,128)(2,1)S(1)}, bf16[1,1024,1280]{2,1,0:T(8,128)(2,1)}, u32[]{:S(2)}) copy-start(bf16[1,1024,1280]{2,1,0:T(8,128)(2,1)} %param.12) | copy-start | bytes 7864324
  29.7 40.3 %all-to-all-start.2 = ((bf16[2,2,262144]{2,1,0:T(2,128)(2,1)}), bf16[2,2,262144]{2,1,0:T(2,128)(2,1)}, u32[]{:S(2)}, u32[]{:S(2)}) async-start(bf16[2,2,262144]{2,1,0:T(2,128)(2,1)} %reshape.58), calls=%async_computation.2 | async-start | bytes 4194304 | tf_op jit(solution)/shard_map/all_to_all | solution.py:20
  70.0 5.8 %copy-start.5 = (bf16[1,1280,1024]{2,1,0:T(8,128)(2,1)S(1)}, bf16[1,1280,1024]{2,1,0:T(8,128)(2,1)}, u32[]{:S(2)}) copy-start(bf16[1,1280,1024]{2,1,0:T(8,128)(2,1)} %param.16) | copy-start | bytes 7864324
  70.0 42.6 %all-to-all-start = ((bf16[2,2,327680]{2,1,0:T(2,128)(2,1)}), bf16[2,2,327680]{2,1,0:T(2,128)(2,1)}, u32[]{:S(2)}, u32[]{:S(2)}) async-start(bf16[2,2,327680]{2,1,0:T(2,128)(2,1)} %reshape.54), calls=%async_computation | async-start | bytes 5242880 | tf_op jit(solution)/shard_map/all_to_all | solution.py:20
  112.6 35.7 %all-to-all-start.1 = ((bf16[2,2,327680]{2,1,0:T(2,128)(2,1)}), bf16[2,2,327680]{2,1,0:T(2,128)(2,1)S(1)}, u32[]{:S(2)}, u32[]{:S(2)}) async-start(bf16[2,2,327680]{2,1,0:T(2,128)(2,1)} %reshape.56), calls=%async_computation.1 | async-start | bytes 5242880 | tf_op jit(solution)/shard_map/all_to_all | solution.py:20
  116.8 174.0 %all-gather.8.cloned.1.call-start = ((), (), s32[]{:S(2)}) async-start(), calls=%async_computation.5 | async-start | bytes 3145728 | tf_op jit(solution)/shard_map/all_gather | solution.py:15
  134.9 1.5 copy-start
  156.2 6.8 %copy-start.14 = (f32[640]{0:T(1024)S(1)}, f32[640]{0:T(1024)}, u32[]{:S(2)}) copy-start(f32[640]{0:T(1024)} %param.18) | copy-start | bytes 7684
  156.2 7.4 %copy-start.17 = (f32[512]{0:T(512)S(1)}, f32[512]{0:T(512)}, u32[]{:S(2)}) copy-start(f32[512]{0:T(512)} %param.22) | copy-start | bytes 6148
  156.2 7.4 %copy-start.18 = (f32[512]{0:T(512)S(1)}, f32[512]{0:T(512)}, u32[]{:S(2)}) copy-start(f32[512]{0:T(512)} %param.14) | copy-start | bytes 6148
  156.2 47.3 %copy-start.13 = (f32[1280]{0:T(1024)S(1)}, f32[1280]{0:T(1024)}, u32[]{:S(2)}) copy-start(f32[1280]{0:T(1024)} %param.15) | copy-start | bytes 15364
  156.2 47.3 %copy-start.15 = (f32[1024]{0:T(1024)S(1)}, f32[1024]{0:T(1024)}, u32[]{:S(2)}) copy-start(f32[1024]{0:T(1024)} %param.19) | copy-start | bytes 12292
  156.2 48.0 %copy-start.16 = (f32[1024]{0:T(1024)S(1)}, f32[1024]{0:T(1024)}, u32[]{:S(2)}) copy-start(f32[1024]{0:T(1024)} %param.23) | copy-start | bytes 12292
  163.6 100.7 %copy-start.9 = (f32[640]{0:T(1024)}, f32[640]{0:T(1024)S(1)}, u32[]{:S(2)}) copy-start(f32[640]{0:T(1024)S(1)} %get-tuple-element.72) | copy-start | bytes 7684
  164.2 86.0 %copy-start.11 = (f32[512]{0:T(512)}, f32[512]{0:T(512)S(1)}, u32[]{:S(2)}) copy-start(f32[512]{0:T(512)S(1)} %get-tuple-element.77) | copy-start | bytes 6148
  164.2 92.6 %copy-start.12 = (f32[512]{0:T(512)}, f32[512]{0:T(512)S(1)}, u32[]{:S(2)}) copy-start(f32[512]{0:T(512)S(1)} %get-tuple-element.67) | copy-start | bytes 6148
  203.5 53.3 %copy-start.7 = (f32[1280]{0:T(1024)}, f32[1280]{0:T(1024)S(1)}, u32[]{:S(2)}) copy-start(f32[1280]{0:T(1024)S(1)} %multiply_add_fusion.3) | copy-start | bytes 15364
  203.5 60.7 %copy-start.10 = (f32[1024]{0:T(1024)}, f32[1024]{0:T(1024)S(1)}, u32[]{:S(2)}) copy-start(f32[1024]{0:T(1024)S(1)} %multiply_add_fusion.5) | copy-start | bytes 12292
  204.2 46.0 %copy-start.8 = (f32[1024]{0:T(1024)}, f32[1024]{0:T(1024)S(1)}, u32[]{:S(2)}) copy-start(f32[1024]{0:T(1024)S(1)} %multiply_add_fusion.4) | copy-start | bytes 12292
  204.2 6.1 %copy-start.2 = (f32[512,1024]{1,0:T(8,128)S(1)}, f32[512,1024]{1,0:T(8,128)}, u32[]{:S(2)}) copy-start(f32[512,1024]{1,0:T(8,128)} %copy-done.1) | copy-start | bytes 6291460
  256.1 75.8 %all-gather.4.cloned.1.call-start = ((), (), s32[]{:S(2)}) async-start(), calls=%async_computation.3 | async-start | bytes 3932160 | tf_op jit(solution)/shard_map/all_gather | solution.py:15
  263.5 109.5 %all-gather.6.cloned.1.call-start = ((), (), s32[]{:S(2)}) async-start(), calls=%async_computation.4 | async-start | bytes 3932160 | tf_op jit(solution)/shard_map/all_gather | solution.py:15
  373.1 3.6 copy-start.3
  376.6 2.5 copy-start.6
  (1 other events, 1.3 us)
Sparse Core Ops, SparseCore 0:
  256.2 34.4 all-gather.7
  292.9 38.9 all-gather.3
  334.0 38.9 all-gather.5
where the time goes:
time: 393 us; the launch traced here: 387 us
  waiting for transfers between devices  114 us (29%)
  other arithmetic  86.1 us (22%)
  blocking collectives  81.4 us (21%)
  local copies, waits for them, and re-layouts  71.9 us (18%)
  between operations  18.3 us (5%)
  starting transfers between devices  15.7 us (4%)
    all_gather x3, waiting for transfers between devices, finish(): lax.all_gather(updated.astype(jnp.bfloat16), 'dp', axis=0, tiled=True)  102 us
    unnamed x51, local copies, waits for them, and re-layouts  62.5 us
    unnamed x3, other arithmetic  55 us
    psum x1, blocking collectives, body(): lax.psum((column_parts[which], jnp.sum(rows_next)), ('dp', 'row'))  38 us
    psum x1, blocking collectives, body(): lax.psum(jnp.sum(update_raw * update_raw), ('dp', 'row', 'col'))  37.2 us
    convert_element_type x3, other arithmetic, finish(): updated.astype(jnp.bfloat16)  18.8 us
    all_to_all x3, starting transfers between devices, reduce_gradient(): lax.all_to_all(gradient, 'dp', split_axis=1, concat_axis=0, tiled=True)  15.4 us
    all_to_all x3, waiting for transfers between devices, reduce_gradient(): lax.all_to_all(gradient, 'dp', split_axis=1, concat_axis=0, tiled=True)  11.3 us
  transfers between devices with their start and end apart: 6, of which 4 were waited for; matrix products, arithmetic and copies ran while one was open for 26% of the time, Pallas kernels for 0%

commit v1 on v0

--- a/solution.py
+++ b/solution.py
@@ -2,6 +2,7 @@
 import jax.numpy as jnp
 from jax import lax
 from jax.sharding import PartitionSpec as P
+from jax.lax import psum
 
 tiny_square = 1e-30
 decay_rate = 0.9
@@ -56,7 +57,15 @@
     for which in range(3):
         row_total = lax.psum(row_parts[which], "col")
         rows_next = decay_rate * groups[which][2] + (1.0 - decay_rate) * row_total / widths[which]
-        column_total, rows_sum = lax.psum((column_parts[which], jnp.sum(rows_next)), ("dp", "row"))
+
+        def expand_record(shard_in):
+            lane_axis = "dp"
+            along_axis = "row"
+            for j in (along_axis, lane_axis):
+                shard_in = psum(shard_in, axis_name=j)
+            return shard_in
+
+        column_total, rows_sum = expand_record((column_parts[which], jnp.sum(rows_next)))
         columns_next = (
             decay_rate * groups[which][3] + (1.0 - decay_rate) * column_total / heights[which]
         )

time: 393 us -> 384 us (0.977)
  blocking collectives: 81.4 us -> 73.8 us
    psum x1 -> x2, blocking collectives: 38 us -> 28.8 us  [expand_record(): shard_in = psum(shard_in, axis_name=j)]
  transfers between devices with their start and end apart: 6 -> 6, of which waited for: 4 -> 4; matrix products, arithmetic and copies ran while one was open for 26% -> 27% of each run, Pallas kernels for 0% -> 0%
where the time goes in v1:
time: 384 us; the launch traced here: 378 us
  waiting for transfers between devices  112 us (29%)
  other arithmetic  86 us (22%)
  blocking collectives  73.8 us (19%)
  local copies, waits for them, and re-layouts  71.9 us (19%)
  between operations  18.3 us (5%)
  starting transfers between devices  15.7 us (4%)
    all_gather x3, waiting for transfers between devices, finish(): lax.all_gather(updated.astype(jnp.bfloat16), 'dp', axis=0, tiled=True)  101 us
    unnamed x51, local copies, waits for them, and re-layouts  62.5 us
    unnamed x3, other arithmetic  55 us
    psum x1, blocking collectives, body(): lax.psum(jnp.sum(update_raw * update_raw), ('dp', 'row', 'col'))  38.8 us
    psum x2, blocking collectives, expand_record(): shard_in = psum(shard_in, axis_name=j)  28.8 us
    convert_element_type x3, other arithmetic, finish(): updated.astype(jnp.bfloat16)  18.8 us
    all_to_all x3, starting transfers between devices, reduce_gradient(): lax.all_to_all(gradient, 'dp', split_axis=1, concat_axis=0, tiled=True)  15.4 us
    all_to_all x3, waiting for transfers between devices, reduce_gradient(): lax.all_to_all(gradient, 'dp', split_axis=1, concat_axis=0, tiled=True)  11.3 us
  transfers between devices with their start and end apart: 6, of which 4 were waited for; matrix products, arithmetic and copies ran while one was open for 27% of the time, Pallas kernels for 0%

profile of v1, /device:TPU:0, one launch (start us, length us, event | category | flops | bytes accessed | tf_op | source)
XLA Modules:
  0.0 378.2 jit_solution(5306693123718397553)
XLA Ops:
  7.2 6.8 %copy.41 = bf16[1,1024,1024]{2,0,1:T(2,128)(2,1)} copy(bf16[1,1024,1024]{2,1,0:T(8,128)(2,1)} %param.20) | data formatting | bytes 4194304 | tf_op args[8]
  14.4 12.8 %reduce.2 = bf16[1024,1024]{1,0:T(8,128)(2,1)S(1)} reduce(bf16[1024,1,1024]{2,1,0:T(2,128)(2,1)} %bitcast.22, bf16[]{:T(256)} %broadcast.37), dimensions={1}, to_apply=%bitcast.17.reduce_sub_computation | reduce | bytes 4194306
  29.7 5.5 %all-to-all-start.2 = ((bf16[2,2,262144]{2,1,0:T(2,128)(2,1)}), bf16[2,2,262144]{2,1,0:T(2,128)(2,1)}, u32[]{:S(2)}, u32[]{:S(2)}) async-start(bf16[2,2,262144]{2,1,0:T(2,128)(2,1)} %reshape.58), calls=%async_computation.2 | async-start | bytes 4194304 | tf_op jit(solution)/shard_map/all_to_all | solution.py:21
  35.2 6.4 %copy.40 = bf16[1,1024,1280]{2,0,1:T(2,128)(2,1)} copy(bf16[1,1024,1280]{2,1,0:T(8,128)(2,1)S(1)} %copy-done.4) | data formatting | bytes 5242880 | tf_op args[0]
  41.6 26.6 %reduce = bf16[1024,1280]{1,0:T(8,128)(2,1)S(1)} reduce(bf16[1024,1,1280]{2,1,0:T(2,128)(2,1)} %bitcast.21, bf16[]{:T(256)} %broadcast.37), dimensions={1}, to_apply=%bitcast.16.reduce_sub_computation | reduce | bytes 5242882
  70.0 5.8 %all-to-all-start = ((bf16[2,2,327680]{2,1,0:T(2,128)(2,1)}), bf16[2,2,327680]{2,1,0:T(2,128)(2,1)}, u32[]{:S(2)}, u32[]{:S(2)}) async-start(bf16[2,2,327680]{2,1,0:T(2,128)(2,1)} %reshape.54), calls=%async_computation | async-start | bytes 5242880 | tf_op jit(solution)/shard_map/all_to_all | solution.py:21
  75.9 18.2 %copy.39 = bf16[1,1280,1024]{2,0,1:T(2,128)(2,1)} copy(bf16[1,1280,1024]{2,1,0:T(8,128)(2,1)S(1)} %copy-done.5) | data formatting | bytes 5242880 | tf_op args[4]
  94.1 15.6 %reduce.1 = bf16[1280,1024]{1,0:T(8,128)(2,1)S(1)} reduce(bf16[1280,1,1024]{2,1,0:T(2,128)(2,1)} %bitcast.18, bf16[]{:T(256)} %broadcast.37), dimensions={1}, to_apply=%bitcast.15.reduce_sub_computation | reduce | bytes 5242882
  112.6 4.1 %all-to-all-start.1 = ((bf16[2,2,327680]{2,1,0:T(2,128)(2,1)}), bf16[2,2,327680]{2,1,0:T(2,128)(2,1)S(1)}, u32[]{:S(2)}, u32[]{:S(2)}) async-start(bf16[2,2,327680]{2,1,0:T(2,128)(2,1)} %reshape.56), calls=%async_computation.1 | async-start | bytes 5242880 | tf_op jit(solution)/shard_map/all_to_all | solution.py:21
  116.9 4.3 %reshape.59 = bf16[1024,1,1024]{2,1,0:T(2,128)(2,1)} reshape(bf16[2,2,262144]{2,1,0:T(2,128)(2,1)} %all-to-all-done.2) | data formatting | bytes 4194304
  126.5 5.1 %reshape.55 = bf16[1024,1,1280]{2,1,0:T(2,128)(2,1)} reshape(bf16[2,2,327680]{2,1,0:T(2,128)(2,1)} %all-to-all-done) | data formatting | bytes 5242880
  137.0 11.3 %all-to-all-done.1 = bf16[2,2,327680]{2,1,0:T(2,128)(2,1)S(1)} async-done(((bf16[2,2,327680]{2,1,0:T(2,128)(2,1)}), bf16[2,2,327680]{2,1,0:T(2,128)(2,1)S(1)}, u32[]{:S(2)}, u32[]{:S(2)}) %all-to-all-start.1) | async-done | bytes 2621472 | tf_op jit(solution)/shard_map/all_to_all | solution.py:21
  148.3 3.7 reshape.57
  156.8 6.2 %all-reduce.1 = (f32[512]{0:T(512)S(1)}, f32[640]{0:T(1024)S(1)}, f32[512]{0:T(512)S(1)}) all-reduce(f32[512]{0:T(512)S(1)} %get-tuple-element.17, f32[640]{0:T(1024)S(1)} %get-tuple-element.15, f32[512]{0:T(512)S(1)} %get-tuple-element.19), channel_id=1, replica_groups=mesh['dp'=2,'row'=4,'col'=4] {'col'}, use_global_device_ids=true, to_apply=%region_2.0 | all-reduce | flops 1664 | bytes 13312 | tf_op jit(solution)/shard_map/psum | solution.py:58
  164.2 20.4 %all-reduce.2 = (f32[1280]{0:T(1024)S(1)}, f32[]{:T(128)}, f32[1024]{0:T(1024)S(1)}, f32[]{:T(128)}, f32[1024]{0:T(1024)S(1)}, /*index=5*/f32[]{:T(128)}) all-reduce(f32[1280]{0:T(1024)S(1)} %get-tuple-element.18, f32[]{:T(128)} %get-tuple-element.54, ...), channel_id=1, replica_groups=mesh['dp'=2,'row'=4,'col'=4] {'row'}, use_global_device_ids=true, to_apply=%region_7.0 | all-reduce | flops 3331 | bytes 26648 | tf_op jit(solution)/shard_map/psum | solution.py:65
  184.6 8.3 %all-reduce.3 = (f32[1280]{0:T(1024)S(1)}, f32[]{:T(128)}, f32[1024]{0:T(1024)S(1)}, f32[]{:T(128)}, f32[1024]{0:T(1024)S(1)}, /*index=5*/f32[]{:T(128)}) all-reduce(f32[1280]{0:T(1024)S(1)} %get-tuple-element.27, f32[]{:T(128)} %get-tuple-element.28, f32[1024]{0:T(1024)S(1)} %get-tuple-element.29, ...), channel_id=1, replica_groups=mesh['dp'=2,'row'=4,'col'=4] {'dp'}, use_global_device_ids=true, to_apply=%region_8.0 | all-reduce | flops 3331 | bytes 26648 | tf_op jit(solution)/shard_map/psum | solution.py:65
  195.0 3.8 multiply_reduce_fusion.1
  203.0 38.8 %all-reduce = (f32[]{:T(128)}, f32[]{:T(128)}, f32[]{:T(128)}) all-reduce(f32[]{:T(128)} %multiply_reduce_fusion.1, f32[]{:T(128)} %multiply_reduce_fusion, f32[]{:T(128)} %multiply_reduce_fusion.2), channel_id=1, replica_groups=mesh['dp'=2,'row'=4,'col'=4] {'dp','row','col'}, use_global_device_ids=true, to_apply=%region_10.0 | all-reduce | flops 3 | bytes 24 | tf_op jit(solution)/shard_map/psum | solution.py:76
  242.6 5.9 %fusion.6 = (bf16[512,1024]{1,0:T(8,128)(2,1)}, f32[512,1024]{1,0:T(8,128)}, f32[512,1024]{1,0:T(8,128)}) fusion(f32[512,1024]{1,0:T(8,128)} %param.21, f32[]{:T(128)S(6)} %max.11, f32[1024]{0:T(1024)S(1)} %multiply_add_fusion.4, f32[512]{0:T(512)S(1)} %get-tuple-element.83, f32[]{:T(128)S(6)} %div.136, f32[512,1024]{1,0:T(8,128)} %copy-done.1), kind=kLoop, calls=%fused_computation.30 | loop fusion | flops 4194304 | bytes 9443336 | tf_op jit(solution)/shard_map/convert_element_type | solution.py:16
  249.2 6.7 %fusion.8 = (bf16[512,1280]{1,0:T(8,128)(2,1)}, f32[512,1280]{1,0:T(8,128)}, f32[512,1280]{1,0:T(8,128)}) fusion(f32[512,1280]{1,0:T(8,128)} %param.13, f32[]{:T(128)S(6)} %max.9, f32[1280]{0:T(1024)S(1)} %multiply_add_fusion.3, f32[512]{0:T(512)S(1)} %get-tuple-element.73, f32[]{:T(128)S(6)} %div.112, f32[512,1280]{1,0:T(8,128)} %copy-done), kind=kLoop, calls=%fused_computation.32 | loop fusion | flops 5242880 | bytes 11803656 | tf_op jit(solution)/shard_map/convert_element_type | solution.py:16
  256.7 6.2 %fusion.7 = (bf16[640,1024]{1,0:T(8,128)(2,1)}, f32[640,1024]{1,0:T(8,128)}, f32[640,1024]{1,0:T(8,128)}) fusion(f32[640,1024]{1,0:T(8,128)} %param.17, f32[]{:T(128)S(6)} %max.10, f32[1024]{0:T(1024)S(1)} %multiply_add_fusion.5, f32[640]{0:T(1024)S(1)} %get-tuple-element.78, f32[]{:T(128)S(6)} %div.124, f32[640,1024]{1,0:T(8,128)S(1)} %convert_reduce_fusion), kind=kLoop, calls=%fused_computation.31 | loop fusion | flops 5242880 | bytes 11803144 | tf_op jit(solution)/shard_map/convert_element_type | solution.py:16
  262.9 18.8 %all-gather.8.cloned.1.call-done = bf16[1024,1024]{1,0:T(8,128)(2,1)} async-done(((bf16[512,1024]{1,0:T(8,128)(2,1)}), bf16[1024,1024]{1,0:T(8,128)(2,1)}) %all-gather.8.cloned.1.call-update) | async-done | bytes 2097168 | tf_op jit(solution)/shard_map/all_gather | solution.py:16
  281.7 41.1 %all-gather.4.cloned.1.call-done = bf16[1024,1280]{1,0:T(8,128)(2,1)} async-done(((bf16[512,1280]{1,0:T(8,128)(2,1)}), bf16[1024,1280]{1,0:T(8,128)(2,1)}) %all-gather.4.cloned.1.call-update) | async-done | bytes 2621456 | tf_op jit(solution)/shard_map/all_gather | solution.py:16
  322.9 41.2 %all-gather.6.cloned.1.call-done = bf16[1280,1024]{1,0:T(8,128)(2,1)} async-done(((bf16[640,1024]{1,0:T(8,128)(2,1)}), bf16[1280,1024]{1,0:T(8,128)(2,1)}) %all-gather.6.cloned.1.call-update) | async-done | bytes 2621456 | tf_op jit(solution)/shard_map/all_gather | solution.py:16
  (69 shorter events, 36.4 us)
Async XLA Ops:
  29.7 5.5 %copy-start.4 = (bf16[1,1024,1280]{2,1,0:T(8,128)(2,1)S(1)}, bf16[1,1024,1280]{2,1,0:T(8,128)(2,1)}, u32[]{:S(2)}) copy-start(bf16[1,1024,1280]{2,1,0:T(8,128)(2,1)} %param.12) | copy-start | bytes 7864324
  29.7 40.3 %all-to-all-start.2 = ((bf16[2,2,262144]{2,1,0:T(2,128)(2,1)}), bf16[2,2,262144]{2,1,0:T(2,128)(2,1)}, u32[]{:S(2)}, u32[]{:S(2)}) async-start(bf16[2,2,262144]{2,1,0:T(2,128)(2,1)} %reshape.58), calls=%async_computation.2 | async-start | bytes 4194304 | tf_op jit(solution)/shard_map/all_to_all | solution.py:21
  70.0 5.8 %copy-start.5 = (bf16[1,1280,1024]{2,1,0:T(8,128)(2,1)S(1)}, bf16[1,1280,1024]{2,1,0:T(8,128)(2,1)}, u32[]{:S(2)}) copy-start(bf16[1,1280,1024]{2,1,0:T(8,128)(2,1)} %param.16) | copy-start | bytes 7864324
  70.0 42.6 %all-to-all-start = ((bf16[2,2,327680]{2,1,0:T(2,128)(2,1)}), bf16[2,2,327680]{2,1,0:T(2,128)(2,1)}, u32[]{:S(2)}, u32[]{:S(2)}) async-start(bf16[2,2,327680]{2,1,0:T(2,128)(2,1)} %reshape.54), calls=%async_computation | async-start | bytes 5242880 | tf_op jit(solution)/shard_map/all_to_all | solution.py:21
  112.6 35.7 %all-to-all-start.1 = ((bf16[2,2,327680]{2,1,0:T(2,128)(2,1)}), bf16[2,2,327680]{2,1,0:T(2,128)(2,1)S(1)}, u32[]{:S(2)}, u32[]{:S(2)}) async-start(bf16[2,2,327680]{2,1,0:T(2,128)(2,1)} %reshape.56), calls=%async_computation.1 | async-start | bytes 5242880 | tf_op jit(solution)/shard_map/all_to_all | solution.py:21
  116.8 165.0 %all-gather.8.cloned.1.call-start = ((), (), s32[]{:S(2)}) async-start(), calls=%async_computation.5 | async-start | bytes 3145728 | tf_op jit(solution)/shard_map/all_gather | solution.py:16
  134.9 1.5 copy-start
  156.2 6.8 %copy-start.14 = (f32[640]{0:T(1024)S(1)}, f32[640]{0:T(1024)}, u32[]{:S(2)}) copy-start(f32[640]{0:T(1024)} %param.18) | copy-start | bytes 7684
  156.2 7.4 %copy-start.17 = (f32[512]{0:T(512)S(1)}, f32[512]{0:T(512)}, u32[]{:S(2)}) copy-start(f32[512]{0:T(512)} %param.22) | copy-start | bytes 6148
  156.2 7.4 %copy-start.18 = (f32[512]{0:T(512)S(1)}, f32[512]{0:T(512)}, u32[]{:S(2)}) copy-start(f32[512]{0:T(512)} %param.14) | copy-start | bytes 6148
  156.2 38.1 %copy-start.13 = (f32[1280]{0:T(1024)S(1)}, f32[1280]{0:T(1024)}, u32[]{:S(2)}) copy-start(f32[1280]{0:T(1024)} %param.15) | copy-start | bytes 15364
  156.2 38.1 %copy-start.15 = (f32[1024]{0:T(1024)S(1)}, f32[1024]{0:T(1024)}, u32[]{:S(2)}) copy-start(f32[1024]{0:T(1024)} %param.19) | copy-start | bytes 12292
  156.2 38.8 %copy-start.16 = (f32[1024]{0:T(1024)S(1)}, f32[1024]{0:T(1024)}, u32[]{:S(2)}) copy-start(f32[1024]{0:T(1024)} %param.23) | copy-start | bytes 12292
  163.6 93.1 %copy-start.9 = (f32[640]{0:T(1024)}, f32[640]{0:T(1024)S(1)}, u32[]{:S(2)}) copy-start(f32[640]{0:T(1024)S(1)} %get-tuple-element.78) | copy-start | bytes 7684
  164.2 78.4 %copy-start.11 = (f32[512]{0:T(512)}, f32[512]{0:T(512)S(1)}, u32[]{:S(2)}) copy-start(f32[512]{0:T(512)S(1)} %get-tuple-element.83) | copy-start | bytes 6148
  164.2 85.0 %copy-start.12 = (f32[512]{0:T(512)}, f32[512]{0:T(512)S(1)}, u32[]{:S(2)}) copy-start(f32[512]{0:T(512)S(1)} %get-tuple-element.73) | copy-start | bytes 6148
  194.3 55.0 %copy-start.7 = (f32[1280]{0:T(1024)}, f32[1280]{0:T(1024)S(1)}, u32[]{:S(2)}) copy-start(f32[1280]{0:T(1024)S(1)} %multiply_add_fusion.3) | copy-start | bytes 15364
  194.3 62.4 %copy-start.10 = (f32[1024]{0:T(1024)}, f32[1024]{0:T(1024)S(1)}, u32[]{:S(2)}) copy-start(f32[1024]{0:T(1024)S(1)} %multiply_add_fusion.5) | copy-start | bytes 12292
  195.0 47.6 %copy-start.8 = (f32[1024]{0:T(1024)}, f32[1024]{0:T(1024)S(1)}, u32[]{:S(2)}) copy-start(f32[1024]{0:T(1024)S(1)} %multiply_add_fusion.4) | copy-start | bytes 12292
  195.0 6.1 %copy-start.2 = (f32[512,1024]{1,0:T(8,128)S(1)}, f32[512,1024]{1,0:T(8,128)}, u32[]{:S(2)}) copy-start(f32[512,1024]{1,0:T(8,128)} %copy-done.1) | copy-start | bytes 6291460
  248.5 74.4 %all-gather.4.cloned.1.call-start = ((), (), s32[]{:S(2)}) async-start(), calls=%async_computation.3 | async-start | bytes 3932160 | tf_op jit(solution)/shard_map/all_gather | solution.py:16
  255.9 108.1 %all-gather.6.cloned.1.call-start = ((), (), s32[]{:S(2)}) async-start(), calls=%async_computation.4 | async-start | bytes 3932160 | tf_op jit(solution)/shard_map/all_gather | solution.py:16
  364.0 3.6 copy-start.3
  367.6 2.5 copy-start.6
  (1 other events, 1.3 us)
Sparse Core Ops, SparseCore 0:
  248.6 33.0 all-gather.7
  283.8 38.9 all-gather.3
  325.0 38.9 all-gather.5
